TPU v7x, 32 devices: a whole 2x2x4 slice. The times are simulated.
32 devices in a mesh: seq: 8 (over z, y), head: 4 (over x, core).
Axes of the slice: x: 2, y: 2, z: 4, core: 2. Of those that a mesh axis runs over, the one named last changes fastest.
Arguments:
- queries: float32 [1024, 8192], P('seq', 'head'), may hold values from -48 to 48
- prefix_keys: float32 [5120, 512], P('seq', 'head'), may hold values from -5 to 5
- prefix_value_rows: float32 [5120, 512], P('seq', 'head'), may hold values from -6 to 6
- response_keys: float32 [1024, 512], P('seq', 'head'), may hold values from -6 to 6
- response_values: float32 [1024, 512], P('seq', 'head'), may hold values from -6 to 6
- out_grad: float32 [1024, 8192], P('seq', 'head'), may hold values from -6 to 6
- lengths: int32 [8], P('seq'), may hold values from 32 to 128
Outputs:
- grad_queries: float32 [1024, 8192], P(('seq', 'head'))
- grad_prefix_keys: float32 [5120, 512], P('seq', 'head')
- grad_prefix_values: float32 [5120, 512], P('seq', 'head')
- grad_resp_keys: float32 [1024, 512], P('seq', 'head')
- grad_resp_values: float32 [1024, 512], P('seq', 'head')
All inputs are finite; a program needn't handle non-finite values.
Results may differ from a plain program's by a relative error of at most 0.0003.
Values sent between devices are 32-bit elements; how exact they have to be, the bound alone decides.
A program may use at most 128 MiB of HBM per device.

v0:
```python
import functools
import math

import jax
import jax.numpy as jnp
from jax import lax
from jax.experimental import pallas as pl
from jax.experimental.pallas import tpu as pltpu
from jax.sharding import PartitionSpec as P

HEAD_SIZE = 128
WINDOW = 3
D = HEAD_SIZE
MESH = pl.DeviceIdType.MESH
F32, BF16 = jnp.float32, jnp.bfloat16
SUB = 128
UNROLL = 4


def split(x):
    hi = x.astype(BF16)
    lo = (x - hi.astype(F32)).astype(BF16)
    return hi, lo


def dot(a, b):
    return jnp.dot(a, b, preferred_element_type=F32)


def chunk_of(block):
    return (block // SUB + 1) // 2 * SUB


def kernel(
    n_seq, n_head,
    length_ref, q_hbm, pk_ref, pv_ref, rk_ref, rv_ref, g_hbm,
    gq_ref, gpk_ref, gpv_ref, grk_ref, grv_ref,
    q_ref, g_ref, kv0, kv1, kv2, kvr, kc, vc, kt, qt, gt, qr, gr, s_ref, dp_ref, m_ref, l_ref, d_ref,
    pcat, dcat, dk_acc, dv_acc, dqt, dqs, ry, rz,
    in_z_send, in_z_recv, in_y_send, in_y_recv,
    out_z_send, out_z_recv, out_y_send, out_y_recv,
    q_send, q_recv, q_local, load_sem,
):
    rows = q_hbm.shape[0]
    heads = q_hbm.shape[1] // D
    pairs = heads // 2
    block = pk_ref.shape[0]
    big = chunk_of(block)
    spans = ((0, big), (big, block - big))
    lead = block + rows
    off1, off2 = lead, lead + block
    factor = D ** (-0.5)
    seq = lax.axis_index("seq")
    head = lax.axis_index("head")
    even = lax.rem(seq, 2) == 0
    odd = jnp.logical_not(even)
    partner = seq + 1 - 2 * lax.rem(seq, 2)
    below = lax.rem(seq + n_seq - 2, n_seq)
    above = lax.rem(seq + 2, n_seq)

    barrier = pltpu.get_barrier_semaphore()
    for other in (partner, below, above):
        pl.semaphore_signal(barrier, inc=1, device_id=(other, head), device_id_type=MESH)
    for step in range(1, n_head):
        pl.semaphore_signal(
            barrier, inc=1, device_id=(seq, lax.rem(head + step, n_head)), device_id_type=MESH
        )
    loads = [
        pltpu.make_async_copy(src, dst, load_sem.at[i])
        for i, (src, dst) in enumerate(
            (
                (pk_ref, kv0.at[0]),
                (pv_ref, kv0.at[1]),
                (rk_ref, kvr.at[0]),
                (rv_ref, kvr.at[1]),
                (q_hbm, q_ref),
                (g_hbm, g_ref),
            )
        )
    ]
    for load in loads:
        load.start()
    pl.semaphore_wait(barrier, 3 + n_head - 1)

    def remote(src, dst, send, recv, to):
        return pltpu.make_async_remote_copy(
            src_ref=src, dst_ref=dst, send_sem=send, recv_sem=recv,
            device_id=to, device_id_type=MESH,
        )

    pieces = [(c, t) for c in range(2) for t in range(2)]
    own = (pk_ref, pv_ref)

    def at(c):
        return pl.ds(*spans[c])

    def in_z(c, t):
        return remote(own[t].at[at(c)], kv2.at[t, at(c)], in_z_send.at[c, t], in_z_recv.at[c, t], (below, head))

    def in_y_own(c, t):
        return remote(own[t].at[at(c)], kv1.at[t, at(c)], in_y_send.at[c, t], in_y_recv.at[c, t], (partner, head))

    def in_y_pass(c, t):
        return remote(kv2.at[t, at(c)], kv1.at[t, at(c)], in_y_send.at[c, t], in_y_recv.at[c, t], (partner, head))

    for c, t in pieces:
        in_z(c, t).start()

    @pl.when(odd)
    def _():
        for c, t in pieces:
            in_y_own(c, t).start()

    def place(keys, values, first, offset, size):
        for start in range(0, size, SUB):
            here = pl.ds(offset + start, SUB)
            k = keys[pl.ds(first + start, SUB), :]
            hi, lo = split(k)
            kc[here, 0:D] = hi
            kc[here, D : 2 * D] = lo
            kc[here, 2 * D : 3 * D] = hi
            hi, lo = split(k.T)
            kt[0:D, here] = hi
            kt[D : 2 * D, here] = lo
            hi, lo = split(values[pl.ds(first + start, SUB), :])
            vc[here, 0:D] = hi
            vc[here, D : 2 * D] = lo
            vc[here, 2 * D : 3 * D] = hi

    for load in loads[:4]:
        load.wait()
    place(kv0.at[0], kv0.at[1], 0, 0, block)
    place(kvr.at[0], kvr.at[1], 0, block, rows)
    for load in loads[4:]:
        load.wait()

    length = length_ref[0]
    token = lax.broadcasted_iota(jnp.int32, (rows, 1), 0)
    live = token < length
    for h in range(heads):
        cols = pl.ds(h * D, D)
        pair, half = h // 2, h % 2
        lanes = pl.ds(half * rows, rows)
        q = q_ref[:, cols]
        g = jnp.where(live, g_ref[:, cols], 0.0)
        for x, wide, tall, scale in (
            (q, qr, qt, factor * math.log2(math.e)),
            (g, gr, gt, 1.0),
        ):
            hi, lo = split((x * scale).T)
            tall[pair, 0:D, lanes] = hi
            tall[pair, D : 2 * D, lanes] = hi
            tall[pair, 2 * D : 3 * D, lanes] = lo
            hi, lo = split(x * factor) if wide is qr else split(x)
            for copy in range(2):
                at_rows = pl.ds(copy * 2 * rows + half * rows, rows)
                wide[pair, at_rows, 0:D] = hi
                wide[pair, at_rows, D : 2 * D] = lo

    def scores(offset, size, first):
        def products(pair):
            s = dot(kc[pl.ds(offset, size), :], qt[pair])
            if first:
                slot = lax.broadcasted_iota(jnp.int32, (rows, 2 * rows), 0)
                lane = lax.broadcasted_iota(jnp.int32, (rows, 2 * rows), 1)
                query = jnp.where(lane >= rows, lane - rows, lane)
                visible = (slot <= query) & (slot < length)
                s_ref[pair, pl.ds(offset, block), :] = s[:block]
                s_ref[pair, pl.ds(offset + block, rows), :] = jnp.where(visible, s[block:], -1e30)
            else:
                s_ref[pair, pl.ds(offset, size), :] = s
            dp_ref[pair, pl.ds(offset, size), :] = dot(vc[pl.ds(offset, size), :], gt[pair])

        def sums(pair):
            top = None
            for start in range(0, size, SUB):
                part = jnp.max(
                    s_ref[pair, pl.ds(offset + start, SUB), :].reshape(SUB // 8, 8, 2 * rows), axis=0
                )
                top = part if top is None else jnp.maximum(top, part)
            top = jnp.max(top, axis=0, keepdims=True)
            total = jnp.zeros((8, 2 * rows), F32)
            dsum = jnp.zeros((8, 2 * rows), F32)
            for start in range(0, size, SUB):
                here = pl.ds(offset + start, SUB)
                e = jnp.exp2(s_ref[pair, here, :] - top)
                total = total + jnp.sum(e.reshape(SUB // 8, 8, 2 * rows), axis=0)
                dsum = dsum + jnp.sum((e * dp_ref[pair, here, :]).reshape(SUB // 8, 8, 2 * rows), axis=0)
            total = jnp.sum(total, axis=0, keepdims=True)
            dsum = jnp.sum(dsum, axis=0, keepdims=True)
            if first:
                m_ref[pair] = top
                l_ref[pair] = total
                d_ref[pair] = dsum
            else:
                newest = jnp.maximum(m_ref[pair], top)
                fade, add = jnp.exp2(m_ref[pair] - newest), jnp.exp2(top - newest)
                m_ref[pair] = newest
                l_ref[pair] = l_ref[pair] * fade + total * add
                d_ref[pair] = d_ref[pair] * fade + dsum * add

        def body(i, carry):
            for j in range(UNROLL):
                products(i * UNROLL + j)
                if j:
                    sums(i * UNROLL + j - 1)
            sums(i * UNROLL + UNROLL - 1)
            return carry

        lax.fori_loop(0, pairs // UNROLL, body, 0)

    def grads(offset, size, first, begin=0, end=None, then=None):
        keys = pl.ds(offset, size)
        if begin == 0:
            dk_acc[keys, :] = jnp.zeros((size, D), F32)
            dv_acc[keys, :] = jnp.zeros((size, D), F32)
        some = pl.ds(0, size)

        def weights(pair, slot):
            shift, mean = m_ref[pair], d_ref[pair]
            for start in range(0, size, SUB):
                here = pl.ds(offset + start, SUB)
                p = jnp.exp2(s_ref[pair, here, :] - shift)
                ds = p * (dp_ref[pair, here, :] - mean)
                to = pl.ds(start, SUB)
                hi, lo = split(p)
                pcat[slot, to, 0 : 2 * rows] = hi
                pcat[slot, to, 2 * rows :] = lo
                hi, lo = split(ds)
                dcat[slot, to, 0 : 2 * rows] = hi
                dcat[slot, to, 2 * rows :] = lo

        def products(pair, slot):
            dv = dot(pcat[slot, some, :], gr[pair])
            dv_acc[keys, :] += dv[:, :D] + dv[:, D:]
            dk = dot(dcat[slot, some, :], qr[pair])
            dk_acc[keys, :] += dk[:, :D] + dk[:, D:]
            high = dot(kt[:, keys], dcat[slot, some, 0 : 2 * rows])
            dq = high[:D] + high[D:] + dot(kt[0:D, keys], dcat[slot, some, 2 * rows :])
            if first:
                dqt[pair] = dq
            elif then is None:
                dqt[pair] += dq
            else:
                then(pair, dqt[pair] + dq)

        def body(i, carry):
            weights(2 * i, 0)
            weights(2 * i + 1, 1)
            products(2 * i, 0)
            products(2 * i + 1, 1)
            return carry

        lax.fori_loop(begin // 2, (pairs if end is None else end) // 2, body, 0)

    scores(0, lead, True)
    for c in range(2):
        for t in range(2):
            in_z(c, t).wait_recv()

            @pl.when(even)
            def _():
                in_y_pass(c, t).start()

        place(kv2.at[0], kv2.at[1], spans[c][0], off2 + spans[c][0], spans[c][1])
        scores(off2 + spans[c][0], spans[c][1], False)
        for t in range(2):
            in_y_own(c, t).wait_recv()
        place(kv1.at[0], kv1.at[1], spans[c][0], off1 + spans[c][0], spans[c][1])
        scores(off1 + spans[c][0], spans[c][1], False)

    def finish(pair, carry):
        l = l_ref[pair]
        d_ref[pair] = d_ref[pair] / l
        m_ref[pair] = m_ref[pair] + jnp.log2(l)
        return carry

    lax.fori_loop(0, pairs, finish, 0)

    acc = (dk_acc, dv_acc)
    parts = block // SUB
    order = list(range(spans[1][0] // SUB, parts)) + list(range(spans[1][0] // SUB))
    split_at = spans[1][1] // SUB

    def out_y(i, t):
        return remote(
            acc[t].at[pl.ds(off1 + i * SUB, SUB)], ry.at[t, pl.ds(i * SUB, SUB)],
            out_y_send.at[i, t], out_y_recv.at[i, t], (partner, head),
        )

    def out_z(i, t):
        return remote(
            acc[t].at[pl.ds(off2 + i * SUB, SUB)], rz.at[t, pl.ds(i * SUB, SUB)],
            out_z_send.at[i, t], out_z_recv.at[i, t], (above, head),
        )

    def send_y(some):
        for i in some:
            for t in range(2):
                out_y(i, t).start()

    def send_z_odd(some):
        @pl.when(odd)
        def _():
            for i in some:
                for t in range(2):
                    out_z(i, t).start()

    def join(some):
        for i in some:
            for t in range(2):
                out_y(i, t).wait_recv()

            @pl.when(even)
            def _():
                for t in range(2):
                    acc[t][pl.ds(off2 + i * SUB, SUB), :] += ry[t, pl.ds(i * SUB, SUB), :]
                for t in range(2):
                    out_z(i, t).start()

    width = heads * D
    share = rows // n_head

    def to_peer(step, pair):
        other = lax.rem(head + step, n_head)
        return remote(
            dqs.at[pair, pl.ds(other * share, share), :],
            gq_ref.at[:, pl.ds(pl.multiple_of(head * width + pair * 2 * D, D), 2 * D)],
            q_send.at[step - 1, pair], q_recv.at[step - 1, pair], (seq, other),
        )

    def keep(pair):
        return pltpu.make_async_copy(
            dqs.at[pair, pl.ds(head * share, share), :],
            gq_ref.at[:, pl.ds(pl.multiple_of(head * width + pair * 2 * D, D), 2 * D)],
            q_local.at[pair],
        )

    def stage(pair, dq):
        for half in range(2):
            dqs[pair, :, half * D : (half + 1) * D] = dq[:, half * rows : (half + 1) * rows].T * factor
        for step in range(1, n_head):
            to_peer(step, pair).start()
        keep(pair).start()

    last, front = spans[1], spans[0]
    grads(off1 + last[0], last[1], True)
    send_y(order[:split_at])
    grads(off2 + last[0], last[1], False)
    send_z_odd(order[:split_at])
    grads(off1 + front[0], front[1], False)
    send_y(order[split_at:])
    join(order[:1])
    grads(off2 + front[0], front[1], False)
    send_z_odd(order[split_at:])
    join(order[1:split_at])
    middle = pairs // 4 * 2
    grads(0, lead, False, 0, middle, stage)
    join(order[split_at : split_at + 1])
    grads(0, lead, False, middle, pairs, stage)
    grk_ref[...] = dk_acc[pl.ds(block, rows), :]
    grv_ref[...] = dv_acc[pl.ds(block, rows), :]
    join(order[split_at + 1 :])

    @pl.when(odd)
    def _():
        for t in range(2):
            acc[t][pl.ds(0, block), :] += ry[t]

    out = (gpk_ref, gpv_ref)
    for i in order:
        for t in range(2):
            here = pl.ds(i * SUB, SUB)
            out_z(i, t).wait_recv()
            out[t][here, :] = acc[t][here, :] + rz[t, here, :]

    for pair in range(pairs):
        keep(pair).wait()
        for step in range(1, n_head):
            to_peer(step, pair).wait()
    for c, t in pieces:
        in_z(c, t).wait_send()
        in_y_own(c, t).wait_send()
    for i in order:
        for t in range(2):
            out_y(i, t).wait_send()
            out_z(i, t).wait_send()


def settle(*refs):
    count = (len(refs) - 2) // 3
    load_sem, store_sem = refs[-2:]
    held = refs[2 * count : 3 * count]
    loads = [
        pltpu.make_async_copy(refs[i], held[i], load_sem.at[i]) for i in range(count)
    ]
    stores = [
        pltpu.make_async_copy(held[i], refs[count + i], store_sem.at[i]) for i in range(count)
    ]
    for load in loads:
        load.start()
    for load, store in zip(loads, stores):
        load.wait()
        store.start()
    for store in stores:
        store.wait()


def per_device(n_seq, n_head, queries, prefix_keys, prefix_value_rows, response_keys, response_values, out_grad, lengths):
    rows, width = queries.shape
    block = prefix_keys.shape[0]
    assert prefix_keys.shape[1] == D
    heads = width // D
    pairs = heads // 2
    keys = WINDOW * block + rows
    lead = block + rows
    vmem = pl.BlockSpec(memory_space=pltpu.VMEM)
    anywhere = pl.BlockSpec(memory_space=pl.ANY)
    sems = pltpu.SemaphoreType.DMA((2, 2))
    part_sems = pltpu.SemaphoreType.DMA((block // SUB, 2))
    shape = jax.ShapeDtypeStruct
    results = pl.pallas_call(
        functools.partial(kernel, n_seq, n_head),
        out_shape=(
            shape((rows // n_head, width * n_head), F32),
            shape((block, D), F32),
            shape((block, D), F32),
            shape((rows, D), F32),
            shape((rows, D), F32),
        ),
        in_specs=[pl.BlockSpec(memory_space=pltpu.SMEM)] + [anywhere] * 6,
        out_specs=(pl.BlockSpec(memory_space=pl.ANY), vmem, vmem, vmem, vmem),
        scratch_shapes=[
            pltpu.VMEM((rows, width), F32),
            pltpu.VMEM((rows, width), F32),
            pltpu.VMEM((2, block, D), F32),
            pltpu.VMEM((2, block, D), F32),
            pltpu.VMEM((2, block, D), F32),
            pltpu.VMEM((2, rows, D), F32),
            pltpu.VMEM((keys, 3 * D), BF16),
            pltpu.VMEM((keys, 3 * D), BF16),
            pltpu.VMEM((2 * D, keys), BF16),
            pltpu.VMEM((pairs, 3 * D, 2 * rows), BF16),
            pltpu.VMEM((pairs, 3 * D, 2 * rows), BF16),
            pltpu.VMEM((pairs, 4 * rows, 2 * D), BF16),
            pltpu.VMEM((pairs, 4 * rows, 2 * D), BF16),
            pltpu.VMEM((pairs, keys, 2 * rows), F32),
            pltpu.VMEM((pairs, keys, 2 * rows), F32),
            pltpu.VMEM((pairs, 1, 2 * rows), F32),
            pltpu.VMEM((pairs, 1, 2 * rows), F32),
            pltpu.VMEM((pairs, 1, 2 * rows), F32),
            pltpu.VMEM((2, lead, 4 * rows), BF16),
            pltpu.VMEM((2, lead, 4 * rows), BF16),
            pltpu.VMEM((keys, D), F32),
            pltpu.VMEM((keys, D), F32),
            pltpu.VMEM((pairs, D, 2 * rows), F32),
            pltpu.VMEM((pairs, rows, 2 * D), F32),
            pltpu.VMEM((2, block, D), F32),
            pltpu.VMEM((2, block, D), F32),
        ]
        + [sems] * 4
        + [part_sems] * 4
        + [pltpu.SemaphoreType.DMA((n_head - 1, pairs))] * 2
        + [pltpu.SemaphoreType.DMA((pairs,)), pltpu.SemaphoreType.DMA((6,))],
        compiler_params=pltpu.CompilerParams(
            collective_id=0, has_side_effects=True, vmem_limit_bytes=63 * 1024 * 1024
        ),
    )(lengths, queries, prefix_keys, prefix_value_rows, response_keys, response_values, out_grad)
    return pl.pallas_call(
        settle,
        out_shape=tuple(shape(x.shape, x.dtype) for x in results),
        in_specs=[anywhere] * len(results),
        out_specs=(anywhere,) * len(results),
        scratch_shapes=[pltpu.VMEM(x.shape, x.dtype) for x in results]
        + [pltpu.SemaphoreType.DMA((len(results),))] * 2,
    )(*results)


def solution(mesh):
    sharded = P("seq", "head")
    return jax.shard_map(
        functools.partial(per_device, mesh.shape["seq"], mesh.shape["head"]),
        mesh=mesh,
        in_specs=(sharded,) * 6 + (P("seq"),),
        out_specs=(P(("seq", "head"), None),) + (sharded,) * 4,
        check_vma=False,
    )
```

profile of v0, /device:TPU:0, one launch (start us, length us, event | category | flops | bytes accessed | tf_op | source)
XLA Modules:
  0.0 59.5 jit_solution(12312639916899991267)
XLA Ops:
  1.3 55.7 %shard_map.110 = (f32[32,8192]{1,0:T(8,128)}, f32[640,128]{1,0:T(8,128)}, f32[640,128]{1,0:T(8,128)}, f32[128,128]{1,0:T(8,128)}, f32[128,128]{1,0:T(8,128)}) custom-call(s32[1]{0:T(128)S(6)} %copy.12.length_ref, f32[128,2048]{1,0:T(8,128)} %q_hbm.1, f32[640,128]{1,0:T(8,128)} %pk_ref.1, f32[640,128]{1,0:T(8,128)} %pv_ref.1, f32[128,128]{1,0:T(8,128)} %rk_ref.1, ...), custom_call_target="tpu_custom_call" | custom-call | tf_op jit(solution)/shard_map/pallas_call | solution.py:422
  57.0 2.5 %shard_map.111 = (f32[32,8192]{1,0:T(8,128)}, f32[640,128]{1,0:T(8,128)}, f32[640,128]{1,0:T(8,128)}, f32[128,128]{1,0:T(8,128)}, f32[128,128]{1,0:T(8,128)}) custom-call(f32[32,8192]{1,0:T(8,128)} %get-tuple-element.10.refs_0_, f32[640,128]{1,0:T(8,128)} %get-tuple-element.11.refs_1_, f32[640,128]{1,0:T(8,128)} %get-tuple-element.12.refs_2_, ...), custom_call_target="tpu_custom_call" | custom-call | tf_op jit(solution)/shard_map/pallas_call | solution.py:469
where the time goes:
time: 59.7 us; the launch traced here: 59.5 us
  Pallas kernels  58.3 us (98%)
  between operations  1.29 us (2%)
    pallas_call x1, Pallas kernels, per_device(): pl.pallas_call(functools.partial(kernel, n_seq, n_head), out_shape=(shape...  55.7 us
    pallas_call x1, Pallas kernels, per_device(): pl.pallas_call(settle, out_shape=tuple((shape(x.shape, x.dtype) for x in...  2.52 us

commit v1 on v0

v1 whole, which is shorter than its diff:
```python
import functools
import math

import jax
import jax.numpy as jnp
from jax import lax
from jax.experimental import pallas as pl
from jax.experimental.pallas import tpu as pltpu
from jax.sharding import PartitionSpec as P

HEAD_SIZE = 128
WINDOW = 3
D = HEAD_SIZE
MESH = pl.DeviceIdType.MESH
F32, BF16 = jnp.float32, jnp.bfloat16
SUB = 128
STEP = 4


def split(x):
    hi = x.astype(BF16)
    lo = (x - hi.astype(F32)).astype(BF16)
    return hi, lo


def dot(a, b):
    return jnp.dot(a, b, preferred_element_type=F32)


def kernel(
    n_seq, n_head,
    length_ref, q_hbm, pk_ref, pv_ref, rk_ref, rv_ref, g_hbm,
    gq_ref, gpk_ref, gpv_ref, grk_ref, grv_ref,
    q_ref, g_ref, kv0, kv1, kv2, kvr, kc, vc, kt, qt, gt, qr, gr, s_ref, dp_ref, m_ref, l_ref, d_ref,
    pcat, dcat, dk_acc, dv_acc, dqt, dqs, ry, rz,
    in_z_send, in_z_recv, in_y_send, in_y_recv,
    out_z_send, out_z_recv, out_y_send, out_y_recv,
    q_send, q_recv, q_local, load_sem,
):
    rows = q_hbm.shape[0]
    heads = q_hbm.shape[1] // D
    pairs = heads // 2
    block = pk_ref.shape[0]
    parts = block // SUB
    lead = block + rows
    cut = (parts + 1) // 2
    front_size, last_at, last_size = cut * SUB, cut * SUB, block - cut * SUB
    off1, off2 = lead, lead + block
    factor = D ** (-0.5)
    seq = lax.axis_index("seq")
    head = lax.axis_index("head")
    even = lax.rem(seq, 2) == 0
    odd = jnp.logical_not(even)
    partner = seq + 1 - 2 * lax.rem(seq, 2)
    below = lax.rem(seq + n_seq - 2, n_seq)
    above = lax.rem(seq + 2, n_seq)

    barrier = pltpu.get_barrier_semaphore()
    for other in (partner, below, above):
        pl.semaphore_signal(barrier, inc=1, device_id=(other, head), device_id_type=MESH)
    for step in range(1, n_head):
        pl.semaphore_signal(
            barrier, inc=1, device_id=(seq, lax.rem(head + step, n_head)), device_id_type=MESH
        )
    loads = [
        pltpu.make_async_copy(src, dst, load_sem.at[i])
        for i, (src, dst) in enumerate(
            (
                (pk_ref, kv0.at[0]),
                (pv_ref, kv0.at[1]),
                (rk_ref, kvr.at[0]),
                (rv_ref, kvr.at[1]),
                (q_hbm, q_ref),
                (g_hbm, g_ref),
            )
        )
    ]
    for load in loads:
        load.start()
    pl.semaphore_wait(barrier, 3 + n_head - 1)

    def remote(src, dst, send, recv, to):
        return pltpu.make_async_remote_copy(
            src_ref=src, dst_ref=dst, send_sem=send, recv_sem=recv,
            device_id=to, device_id_type=MESH,
        )

    own = (pk_ref, pv_ref)

    def piece(i):
        return pl.ds(i * SUB, SUB)

    def in_z(i, t):
        return remote(own[t].at[piece(i)], kv2.at[t, piece(i)], in_z_send.at[i, t], in_z_recv.at[i, t], (below, head))

    def in_y_own(i, t):
        return remote(own[t].at[piece(i)], kv1.at[t, piece(i)], in_y_send.at[i, t], in_y_recv.at[i, t], (partner, head))

    def in_y_pass(i, t):
        return remote(kv2.at[t, piece(i)], kv1.at[t, piece(i)], in_y_send.at[i, t], in_y_recv.at[i, t], (partner, head))

    pieces = [(i, t) for t in range(2) for i in range(parts)]
    for i, t in pieces:
        in_z(i, t).start()

    @pl.when(odd)
    def _():
        for i, t in pieces:
            in_y_own(i, t).start()

    def relay(t, some):
        for i in some:
            in_z(i, t).wait_recv()

            @pl.when(even)
            def _():
                in_y_pass(i, t).start()

    def arrive(t, some):
        for i in some:
            in_y_own(i, t).wait_recv()

    def place_keys(keys, first, offset, size):
        for start in range(0, size, SUB):
            here = pl.ds(offset + start, SUB)
            k = keys[pl.ds(first + start, SUB), :]
            hi, lo = split(k)
            kc[here, 0:D] = hi
            kc[here, D : 2 * D] = lo
            kc[here, 2 * D : 3 * D] = hi
            hi, lo = split(k.T)
            kt[0:D, here] = hi
            kt[D : 2 * D, here] = lo

    def place_values(values, first, offset, size):
        for start in range(0, size, SUB):
            here = pl.ds(offset + start, SUB)
            hi, lo = split(values[pl.ds(first + start, SUB), :])
            vc[here, 0:D] = hi
            vc[here, D : 2 * D] = lo
            vc[here, 2 * D : 3 * D] = hi

    for load in loads[:4]:
        load.wait()
    place_keys(kv0.at[0], 0, 0, block)
    place_values(kv0.at[1], 0, 0, block)
    place_keys(kvr.at[0], 0, block, rows)
    place_values(kvr.at[1], 0, block, rows)
    for load in loads[4:]:
        load.wait()

    length = length_ref[0]
    token = lax.broadcasted_iota(jnp.int32, (rows, 1), 0)
    live = token < length
    for h in range(heads):
        cols = pl.ds(h * D, D)
        pair, half = h // 2, h % 2
        lanes = pl.ds(half * rows, rows)
        q = q_ref[:, cols]
        g = jnp.where(live, g_ref[:, cols], 0.0)
        for x, wide, tall, scale in (
            (q, qr, qt, factor * math.log2(math.e)),
            (g, gr, gt, 1.0),
        ):
            hi, lo = split((x * scale).T)
            tall[pair, 0:D, lanes] = hi
            tall[pair, D : 2 * D, lanes] = hi
            tall[pair, 2 * D : 3 * D, lanes] = lo
            hi, lo = split(x * factor) if wide is qr else split(x)
            for copy in range(2):
                at_rows = pl.ds(copy * 2 * rows + half * rows, rows)
                wide[pair, at_rows, 0:D] = hi
                wide[pair, at_rows, D : 2 * D] = lo

    tile = (SUB // 8, 8, 2 * rows)

    def lead_products(pair):
        s = dot(kc[pl.ds(0, lead), :], qt[pair])
        slot = lax.broadcasted_iota(jnp.int32, (rows, 2 * rows), 0)
        lane = lax.broadcasted_iota(jnp.int32, (rows, 2 * rows), 1)
        query = jnp.where(lane >= rows, lane - rows, lane)
        visible = (slot <= query) & (slot < length)
        s_ref[pair, pl.ds(0, block), :] = s[:block]
        s_ref[pair, pl.ds(block, rows), :] = jnp.where(visible, s[block:], -1e30)
        dp_ref[pair, pl.ds(0, lead), :] = dot(vc[pl.ds(0, lead), :], gt[pair])

    def sums(pair, offset, size, first):
        top = None
        for start in range(0, size, SUB):
            part = jnp.max(s_ref[pair, pl.ds(offset + start, SUB), :].reshape(tile), axis=0)
            top = part if top is None else jnp.maximum(top, part)
        top = jnp.max(top, axis=0, keepdims=True)
        total = jnp.zeros((8, 2 * rows), F32)
        dsum = jnp.zeros((8, 2 * rows), F32)
        for start in range(0, size, SUB):
            here = pl.ds(offset + start, SUB)
            e = jnp.exp2(s_ref[pair, here, :] - top)
            total = total + jnp.sum(e.reshape(tile), axis=0)
            if first:
                dsum = dsum + jnp.sum((e * dp_ref[pair, here, :]).reshape(tile), axis=0)
        if first:
            m_ref[pair] = top
            l_ref[pair] = total
            d_ref[pair] = dsum
        else:
            newest = jnp.maximum(m_ref[pair], top)
            fade, add = jnp.exp2(m_ref[pair] - newest), jnp.exp2(top - newest)
            m_ref[pair] = newest
            l_ref[pair] = l_ref[pair] * fade + total * add
            d_ref[pair] = d_ref[pair] * fade

    def staggered(products, after, unroll, then=None):
        def body(i, carry):
            for j in range(unroll):
                products(i * unroll + j)
                if j:
                    after(i * unroll + j - 1)
            after(i * unroll + unroll - 1)
            if then is not None:
                then(i)
            return carry

        lax.fori_loop(0, pairs // unroll, body, 0)

    def ahead(weights, products, begin, end, step, then=None):
        def body(i, carry):
            first = begin + i * step
            weights(first, 0)
            for j in range(step):
                if j + 1 < step:
                    weights(first + j + 1, (j + 1) % 2)
                products(first + j, j % 2)
            if then is not None:
                then(i)
            return carry

        lax.fori_loop(0, (end - begin) // step, body, 0)

    def key_scores(offset, size):
        def products(pair):
            s_ref[pair, pl.ds(offset, size), :] = dot(kc[pl.ds(offset, size), :], qt[pair])

        staggered(products, lambda pair: sums(pair, offset, size, False), pairs)

    def value_scores(offset, size):
        def products(pair):
            dp_ref[pair, pl.ds(offset, size), :] = dot(vc[pl.ds(offset, size), :], gt[pair])

        def after(pair):
            dsum = d_ref[pair]
            for start in range(0, size, SUB):
                here = pl.ds(offset + start, SUB)
                dsum = dsum + jnp.sum((s_ref[pair, here, :] * dp_ref[pair, here, :]).reshape(tile), axis=0)
            d_ref[pair] = dsum

        staggered(products, after, pairs)

    def value_grads(offset, size, then):
        keys = pl.ds(offset, size)
        dv_acc[keys, :] = jnp.zeros((size, D), F32)
        some = pl.ds(0, size)

        def weights(pair, slot):
            shift = m_ref[pair]
            for start in range(0, size, SUB):
                here = pl.ds(offset + start, SUB)
                p = jnp.exp2(s_ref[pair, here, :] - shift[0:1])
                s_ref[pair, here, :] = p
                to = pl.ds(start, SUB)
                hi, lo = split(p)
                pcat[slot, to, 0 : 2 * rows] = hi
                pcat[slot, to, 2 * rows :] = lo

        def products(pair, slot):
            dv = dot(pcat[slot, some, :], gr[pair])
            dv_acc[keys, :] += dv[:, :D] + dv[:, D:]

        ahead(weights, products, 0, pairs, STEP, then)

    def key_grads(offset, size, first, begin, end):
        keys = pl.ds(offset, size)
        if begin == 0:
            dk_acc[keys, :] = jnp.zeros((size, D), F32)
        some = pl.ds(0, size)

        def weights(pair, slot):
            mean = d_ref[pair][0:1]
            for start in range(0, size, SUB):
                here = pl.ds(offset + start, SUB)
                to = pl.ds(start, SUB)
                hi, lo = split(s_ref[pair, here, :] * (dp_ref[pair, here, :] - mean))
                dcat[slot, to, 0 : 2 * rows] = hi
                dcat[slot, to, 2 * rows :] = lo

        def products(pair, slot):
            dk = dot(dcat[slot, some, :], qr[pair])
            dk_acc[keys, :] += dk[:, :D] + dk[:, D:]
            high = dot(kt[:, keys], dcat[slot, some, 0 : 2 * rows])
            dq = high[:D] + high[D:] + dot(kt[0:D, keys], dcat[slot, some, 2 * rows :])
            if first:
                dqt[pair] = dq
            else:
                dqt[pair] += dq

        ahead(weights, products, begin, end, STEP)

    def lead_grads(begin, end, then):
        size = lead
        keys = some = pl.ds(0, size)
        if begin == 0:
            dk_acc[keys, :] = jnp.zeros((size, D), F32)
            dv_acc[keys, :] = jnp.zeros((size, D), F32)

        def weights(pair, slot):
            shift, mean = m_ref[pair][0:1], d_ref[pair][0:1]
            for start in range(0, size, SUB):
                here = pl.ds(start, SUB)
                p = jnp.exp2(s_ref[pair, here, :] - shift)
                ds = p * (dp_ref[pair, here, :] - mean)
                hi, lo = split(p)
                pcat[slot, here, 0 : 2 * rows] = hi
                pcat[slot, here, 2 * rows :] = lo
                hi, lo = split(ds)
                dcat[slot, here, 0 : 2 * rows] = hi
                dcat[slot, here, 2 * rows :] = lo

        def products(pair, slot):
            dv = dot(pcat[slot, some, :], gr[pair])
            dv_acc[keys, :] += dv[:, :D] + dv[:, D:]
            dk = dot(dcat[slot, some, :], qr[pair])
            dk_acc[keys, :] += dk[:, :D] + dk[:, D:]
            high = dot(kt[:, keys], dcat[slot, some, 0 : 2 * rows])
            dq = high[:D] + high[D:] + dot(kt[0:D, keys], dcat[slot, some, 2 * rows :])
            then(pair, dqt[pair] + dq)

        ahead(weights, products, begin, end, STEP)

    every = range(parts)
    front, last = range(cut), range(cut, parts)
    loops = pairs // STEP

    relay(0, range(1))
    staggered(
        lead_products,
        lambda pair: sums(pair, 0, lead, True),
        STEP,
        lambda i: relay(0, [i + 1]),
    )
    relay(0, range(1 + loops, cut))
    place_keys(kv2.at[0], 0, off2, front_size)
    key_scores(off2, front_size)
    relay(0, range(max(1 + loops, cut), parts))
    place_keys(kv2.at[0], last_at, off2 + last_at, last_size)
    key_scores(off2 + last_at, last_size)
    arrive(0, front)
    place_keys(kv1.at[0], 0, off1, front_size)
    key_scores(off1, front_size)
    relay(1, range(1))
    arrive(0, last)
    place_keys(kv1.at[0], last_at, off1 + last_at, last_size)
    key_scores(off1 + last_at, last_size)
    relay(1, range(1, 2))

    def total(pair, carry):
        l = jnp.sum(l_ref[pair], axis=0, keepdims=True)
        d_ref[pair] = d_ref[pair] / l
        m_ref[pair] = m_ref[pair] + jnp.log2(l)
        return carry

    lax.fori_loop(0, pairs, total, 0)

    acc = (dk_acc, dv_acc)

    def out_y(i, t):
        return remote(
            acc[t].at[pl.ds(off1 + i * SUB, SUB)], ry.at[t, pl.ds(i * SUB, SUB)],
            out_y_send.at[i, t], out_y_recv.at[i, t], (partner, head),
        )

    def out_z(i, t):
        return remote(
            acc[t].at[pl.ds(off2 + i * SUB, SUB)], rz.at[t, pl.ds(i * SUB, SUB)],
            out_z_send.at[i, t], out_z_recv.at[i, t], (above, head),
        )

    def send_y(t, some, when=True):
        @pl.when(when)
        def _():
            for i in some:
                out_y(i, t).start()

    def send_z_odd(t, some):
        @pl.when(odd)
        def _():
            for i in some:
                out_z(i, t).start()

    def join(t, some):
        for i in some:
            out_y(i, t).wait_recv()

            @pl.when(even)
            def _():
                acc[t][pl.ds(off2 + i * SUB, SUB), :] += ry[t, pl.ds(i * SUB, SUB), :]
                out_z(i, t).start()

    width = heads * D
    share = rows // n_head

    def to_peer(step, pair):
        other = lax.rem(head + step, n_head)
        return remote(
            dqs.at[pair, pl.ds(other * share, share), :],
            gq_ref.at[:, pl.ds(pl.multiple_of(head * width + pair * 2 * D, D), 2 * D)],
            q_send.at[step - 1, pair], q_recv.at[step - 1, pair], (seq, other),
        )

    def keep(pair):
        return pltpu.make_async_copy(
            dqs.at[pair, pl.ds(head * share, share), :],
            gq_ref.at[:, pl.ds(pl.multiple_of(head * width + pair * 2 * D, D), 2 * D)],
            q_local.at[pair],
        )

    def stage(pair, dq):
        for half in range(2):
            dqs[pair, :, half * D : (half + 1) * D] = dq[:, half * rows : (half + 1) * rows].T * factor
        for step in range(1, n_head):
            to_peer(step, pair).start()
        keep(pair).start()

    value_grads(off1, block, lambda i: relay(1, [2 + i]))
    send_y(1, every, odd)
    relay(1, range(2 + loops, parts))
    send_y(1, every, even)
    value_grads(off2, block, None)
    send_z_odd(1, every)
    place_values(kv2.at[1], 0, off2, block)
    value_scores(off2, block)
    arrive(1, front)
    place_values(kv1.at[1], 0, off1, front_size)
    value_scores(off1, front_size)
    arrive(1, last)
    place_values(kv1.at[1], last_at, off1 + last_at, last_size)
    value_scores(off1 + last_at, last_size)

    def settle_mean(pair, carry):
        d_ref[pair] = jnp.broadcast_to(jnp.sum(d_ref[pair], axis=0, keepdims=True), (8, 2 * rows))
        return carry

    lax.fori_loop(0, pairs, settle_mean, 0)

    middle = pairs // 2
    key_grads(off1 + last_at, last_size, True, 0, pairs)
    send_y(0, last)
    key_grads(off1, front_size, False, 0, middle)
    key_grads(off2, block, False, 0, middle)
    join(1, every)
    lead_grads(0, middle, stage)
    key_grads(off1, front_size, False, middle, pairs)
    send_y(0, front)
    key_grads(off2, block, False, middle, pairs)
    send_z_odd(0, every)
    join(0, last)
    lead_grads(middle, pairs, stage)
    grk_ref[...] = dk_acc[pl.ds(block, rows), :]
    grv_ref[...] = dv_acc[pl.ds(block, rows), :]
    join(0, front)

    @pl.when(odd)
    def _():
        for t in range(2):
            acc[t][pl.ds(0, block), :] += ry[t]

    out = (gpk_ref, gpv_ref)
    for t in (1, 0):
        for i in (*last, *front):
            here = pl.ds(i * SUB, SUB)
            out_z(i, t).wait_recv()
            out[t][here, :] = acc[t][here, :] + rz[t, here, :]

    for pair in range(pairs):
        keep(pair).wait()
        for step in range(1, n_head):
            to_peer(step, pair).wait()
    for i, t in pieces:
        in_z(i, t).wait_send()
        in_y_own(i, t).wait_send()
        out_y(i, t).wait_send()
        out_z(i, t).wait_send()


def settle(*refs):
    count = (len(refs) - 2) // 3
    load_sem, store_sem = refs[-2:]
    held = refs[2 * count : 3 * count]
    loads = [
        pltpu.make_async_copy(refs[i], held[i], load_sem.at[i]) for i in range(count)
    ]
    stores = [
        pltpu.make_async_copy(held[i], refs[count + i], store_sem.at[i]) for i in range(count)
    ]
    for load in loads:
        load.start()
    for load, store in zip(loads, stores):
        load.wait()
        store.start()
    for store in stores:
        store.wait()


def per_device(n_seq, n_head, queries, prefix_keys, prefix_value_rows, response_keys, response_values, out_grad, lengths):
    rows, width = queries.shape
    block = prefix_keys.shape[0]
    assert prefix_keys.shape[1] == D
    heads = width // D
    pairs = heads // 2
    keys = WINDOW * block + rows
    lead = block + rows
    vmem = pl.BlockSpec(memory_space=pltpu.VMEM)
    anywhere = pl.BlockSpec(memory_space=pl.ANY)
    part_sems = pltpu.SemaphoreType.DMA((block // SUB, 2))
    shape = jax.ShapeDtypeStruct
    results = pl.pallas_call(
        functools.partial(kernel, n_seq, n_head),
        out_shape=(
            shape((rows // n_head, width * n_head), F32),
            shape((block, D), F32),
            shape((block, D), F32),
            shape((rows, D), F32),
            shape((rows, D), F32),
        ),
        in_specs=[pl.BlockSpec(memory_space=pltpu.SMEM)] + [anywhere] * 6,
        out_specs=(pl.BlockSpec(memory_space=pl.ANY), vmem, vmem, vmem, vmem),
        scratch_shapes=[
            pltpu.VMEM((rows, width), F32),
            pltpu.VMEM((rows, width), F32),
            pltpu.VMEM((2, block, D), F32),
            pltpu.VMEM((2, block, D), F32),
            pltpu.VMEM((2, block, D), F32),
            pltpu.VMEM((2, rows, D), F32),
            pltpu.VMEM((keys, 3 * D), BF16),
            pltpu.VMEM((keys, 3 * D), BF16),
            pltpu.VMEM((2 * D, keys), BF16),
            pltpu.VMEM((pairs, 3 * D, 2 * rows), BF16),
            pltpu.VMEM((pairs, 3 * D, 2 * rows), BF16),
            pltpu.VMEM((pairs, 4 * rows, 2 * D), BF16),
            pltpu.VMEM((pairs, 4 * rows, 2 * D), BF16),
            pltpu.VMEM((pairs, keys, 2 * rows), F32),
            pltpu.VMEM((pairs, keys, 2 * rows), F32),
            pltpu.VMEM((pairs, 1, 2 * rows), F32),
            pltpu.VMEM((pairs, 8, 2 * rows), F32),
            pltpu.VMEM((pairs, 8, 2 * rows), F32),
            pltpu.VMEM((2, lead, 4 * rows), BF16),
            pltpu.VMEM((2, lead, 4 * rows), BF16),
            pltpu.VMEM((keys, D), F32),
            pltpu.VMEM((keys, D), F32),
            pltpu.VMEM((pairs, D, 2 * rows), F32),
            pltpu.VMEM((pairs, rows, 2 * D), F32),
            pltpu.VMEM((2, block, D), F32),
            pltpu.VMEM((2, block, D), F32),
        ]
        + [part_sems] * 8
        + [pltpu.SemaphoreType.DMA((n_head - 1, pairs))] * 2
        + [pltpu.SemaphoreType.DMA((pairs,)), pltpu.SemaphoreType.DMA((6,))],
        compiler_params=pltpu.CompilerParams(
            collective_id=0, has_side_effects=True, vmem_limit_bytes=63 * 1024 * 1024
        ),
    )(lengths, queries, prefix_keys, prefix_value_rows, response_keys, response_values, out_grad)
    return pl.pallas_call(
        settle,
        out_shape=tuple(shape(x.shape, x.dtype) for x in results),
        in_specs=[anywhere] * len(results),
        out_specs=(anywhere,) * len(results),
        scratch_shapes=[pltpu.VMEM(x.shape, x.dtype) for x in results]
        + [pltpu.SemaphoreType.DMA((len(results),))] * 2,
    )(*results)


def solution(mesh):
    sharded = P("seq", "head")
    return jax.shard_map(
        functools.partial(per_device, mesh.shape["seq"], mesh.shape["head"]),
        mesh=mesh,
        in_specs=(sharded,) * 6 + (P("seq"),),
        out_specs=(P(("seq", "head"), None),) + (sharded,) * 4,
        check_vma=False,
    )
```

time: 59.7 us -> 56 us (0.938)
  Pallas kernels: 58.3 us -> 54.4 us
    pallas_call x1, Pallas kernels: 55.7 us -> 51.9 us  [per_device(): pl.pallas_call(functools.partial(kernel, n_seq, n_head), out_shape=(shape...]
where the time goes in v1:
time: 56 us; the launch traced here: 55.9 us
  Pallas kernels  54.4 us (97%)
  between operations  1.47 us (3%)
    pallas_call x1, Pallas kernels, per_device(): pl.pallas_call(functools.partial(kernel, n_seq, n_head), out_shape=(shape...  51.9 us
    pallas_call x1, Pallas kernels, per_device(): pl.pallas_call(settle, out_shape=tuple((shape(x.shape, x.dtype) for x in...  2.52 us

profile of v1, /device:TPU:0, one launch (start us, length us, event | category | flops | bytes accessed | tf_op | source)
XLA Modules:
  0.0 55.9 jit_solution(6749072327464289366)
XLA Ops:
  1.3 51.9 %shard_map.110 = (f32[32,8192]{1,0:T(8,128)}, f32[640,128]{1,0:T(8,128)}, f32[640,128]{1,0:T(8,128)}, f32[128,128]{1,0:T(8,128)}, f32[128,128]{1,0:T(8,128)}) custom-call(s32[1]{0:T(128)S(6)} %copy.12.length_ref, f32[128,2048]{1,0:T(8,128)} %q_hbm.1, f32[640,128]{1,0:T(8,128)} %pk_ref.1, f32[640,128]{1,0:T(8,128)} %pv_ref.1, f32[128,128]{1,0:T(8,128)} %rk_ref.1, ...), custom_call_target="tpu_custom_call" | custom-call | tf_op jit(solution)/shard_map/pallas_call | solution.py:524
  53.2 2.5 %shard_map.111 = (f32[32,8192]{1,0:T(8,128)}, f32[640,128]{1,0:T(8,128)}, f32[640,128]{1,0:T(8,128)}, f32[128,128]{1,0:T(8,128)}, f32[128,128]{1,0:T(8,128)}) custom-call(f32[32,8192]{1,0:T(8,128)} %get-tuple-element.10.refs_0_, f32[640,128]{1,0:T(8,128)} %get-tuple-element.11.refs_1_, f32[640,128]{1,0:T(8,128)} %get-tuple-element.12.refs_2_, ...), custom_call_target="tpu_custom_call" | custom-call | tf_op jit(solution)/shard_map/pallas_call | solution.py:570

commit v2 on v1

--- a/solution.py
+++ b/solution.py
@@ -85,7 +85,7 @@
             device_id=to, device_id_type=MESH,
         )
 
-    own = (pk_ref, pv_ref)
+    own = (kv0.at[0], kv0.at[1])
 
     def piece(i):
         return pl.ds(i * SUB, SUB)
@@ -100,6 +100,8 @@
         return remote(kv2.at[t, piece(i)], kv1.at[t, piece(i)], in_y_send.at[i, t], in_y_recv.at[i, t], (partner, head))
 
     pieces = [(i, t) for t in range(2) for i in range(parts)]
+    for load in loads[:2]:
+        load.wait()
     for i, t in pieces:
         in_z(i, t).start()
 
@@ -140,7 +142,7 @@
             vc[here, D : 2 * D] = lo
             vc[here, 2 * D : 3 * D] = hi
 
-    for load in loads[:4]:
+    for load in loads[2:4]:
         load.wait()
     place_keys(kv0.at[0], 0, 0, block)
     place_values(kv0.at[1], 0, 0, block)
@@ -302,42 +304,55 @@
             else:
                 dqt[pair] += dq
 
-        ahead(weights, products, begin, end, STEP)
-
-    def lead_grads(begin, end, then):
-        size = lead
-        keys = some = pl.ds(0, size)
-        if begin == 0:
-            dk_acc[keys, :] = jnp.zeros((size, D), F32)
-            dv_acc[keys, :] = jnp.zeros((size, D), F32)
+        ahead(weights, products, begin, end, STEP if (end - begin) % STEP == 0 else 2)
+
+    def lead_queries(begin, end, then):
+        keys = pl.ds(0, lead)
 
         def weights(pair, slot):
-            shift, mean = m_ref[pair][0:1], d_ref[pair][0:1]
-            for start in range(0, size, SUB):
+            shift, mean = m_ref[pair], d_ref[pair][0:1]
+            for start in range(0, lead, SUB):
                 here = pl.ds(start, SUB)
                 p = jnp.exp2(s_ref[pair, here, :] - shift)
                 ds = p * (dp_ref[pair, here, :] - mean)
-                hi, lo = split(p)
-                pcat[slot, here, 0 : 2 * rows] = hi
-                pcat[slot, here, 2 * rows :] = lo
+                s_ref[pair, here, :] = p
+                dp_ref[pair, here, :] = ds
                 hi, lo = split(ds)
                 dcat[slot, here, 0 : 2 * rows] = hi
                 dcat[slot, here, 2 * rows :] = lo
 
         def products(pair, slot):
-            dv = dot(pcat[slot, some, :], gr[pair])
-            dv_acc[keys, :] += dv[:, :D] + dv[:, D:]
-            dk = dot(dcat[slot, some, :], qr[pair])
-            dk_acc[keys, :] += dk[:, :D] + dk[:, D:]
-            high = dot(kt[:, keys], dcat[slot, some, 0 : 2 * rows])
-            dq = high[:D] + high[D:] + dot(kt[0:D, keys], dcat[slot, some, 2 * rows :])
+            high = dot(kt[:, keys], dcat[slot, :, 0 : 2 * rows])
+            dq = high[:D] + high[D:] + dot(kt[0:D, keys], dcat[slot, :, 2 * rows :])
             then(pair, dqt[pair] + dq)
 
-        ahead(weights, products, begin, end, STEP)
-
-    every = range(parts)
-    front, last = range(cut), range(cut, parts)
+        ahead(weights, products, begin, end, 2)
+
+    def lead_grads(then):
+        dk_acc[pl.ds(0, lead), :] = jnp.zeros((lead, D), F32)
+        dv_acc[pl.ds(0, lead), :] = jnp.zeros((lead, D), F32)
+
+        def weights(pair, slot):
+            for start in range(0, lead, SUB):
+                here = pl.ds(start, SUB)
+                hi, lo = split(s_ref[pair, here, :])
+                pcat[slot, here, 0 : 2 * rows] = hi
+                pcat[slot, here, 2 * rows :] = lo
+                hi, lo = split(dp_ref[pair, here, :])
+                dcat[slot, here, 0 : 2 * rows] = hi
+                dcat[slot, here, 2 * rows :] = lo
+
+        def products(pair, slot):
+            dv = dot(pcat[slot], gr[pair])
+            dv_acc[pl.ds(0, lead), :] += dv[:, :D] + dv[:, D:]
+            dk = dot(dcat[slot], qr[pair])
+            dk_acc[pl.ds(0, lead), :] += dk[:, :D] + dk[:, D:]
+
+        ahead(weights, products, 0, pairs, 2, then)
+
+    every, front, last = range(parts), range(cut), range(cut, parts)
     loops = pairs // STEP
+    assert cut - 1 <= pairs // 2 and parts > 1 + loops
 
     relay(0, range(1))
     staggered(
@@ -440,6 +455,7 @@
     arrive(1, front)
     place_values(kv1.at[1], 0, off1, front_size)
     value_scores(off1, front_size)
+    join(1, range(1))
     arrive(1, last)
     place_values(kv1.at[1], last_at, off1 + last_at, last_size)
     value_scores(off1 + last_at, last_size)
@@ -450,22 +466,29 @@
 
     lax.fori_loop(0, pairs, settle_mean, 0)
 
-    middle = pairs // 2
+    quarter = pairs // 4
     key_grads(off1 + last_at, last_size, True, 0, pairs)
     send_y(0, last)
-    key_grads(off1, front_size, False, 0, middle)
-    key_grads(off2, block, False, 0, middle)
-    join(1, every)
-    lead_grads(0, middle, stage)
-    key_grads(off1, front_size, False, middle, pairs)
+    join(1, range(1, 3))
+    key_grads(off1, front_size, False, 0, pairs)
     send_y(0, front)
-    key_grads(off2, block, False, middle, pairs)
+    join(1, range(3, parts))
+    key_grads(off2, block, False, 0, quarter)
+    lead_queries(0, quarter, stage)
+    key_grads(off2, block, False, quarter, pairs)
     send_z_odd(0, every)
     join(0, last)
-    lead_grads(middle, pairs, stage)
+    lead_queries(quarter, pairs, stage)
+    join(0, range(1))
+
+    def join_front(i):
+        @pl.when(i < cut - 1)
+        def _():
+            join(0, [i + 1])
+
+    lead_grads(join_front)
     grk_ref[...] = dk_acc[pl.ds(block, rows), :]
     grv_ref[...] = dv_acc[pl.ds(block, rows), :]
-    join(0, front)
 
     @pl.when(odd)
     def _():
@@ -474,7 +497,7 @@
 
     out = (gpk_ref, gpv_ref)
     for t in (1, 0):
-        for i in (*last, *front):
+        for i in every:
             here = pl.ds(i * SUB, SUB)
             out_z(i, t).wait_recv()
             out[t][here, :] = acc[t][here, :] + rz[t, here, :]
@@ -491,19 +514,12 @@
 
 
 def settle(*refs):
-    count = (len(refs) - 2) // 3
-    load_sem, store_sem = refs[-2:]
-    held = refs[2 * count : 3 * count]
-    loads = [
-        pltpu.make_async_copy(refs[i], held[i], load_sem.at[i]) for i in range(count)
+    count = (len(refs) - 1) // 2
+    store_sem = refs[-1]
+    stores = [
+        pltpu.make_async_copy(refs[i], refs[count + i], store_sem.at[i]) for i in range(count)
     ]
-    stores = [
-        pltpu.make_async_copy(held[i], refs[count + i], store_sem.at[i]) for i in range(count)
-    ]
-    for load in loads:
-        load.start()
-    for load, store in zip(loads, stores):
-        load.wait()
+    for store in stores:
         store.start()
     for store in stores:
         store.wait()
@@ -524,14 +540,14 @@
     results = pl.pallas_call(
         functools.partial(kernel, n_seq, n_head),
         out_shape=(
-            shape((rows // n_head, width * n_head), F32),
-            shape((block, D), F32),
-            shape((block, D), F32),
-            shape((rows, D), F32),
-            shape((rows, D), F32),
+            pltpu.VMEM((rows // n_head, width * n_head), F32),
+            pltpu.VMEM((block, D), F32),
+            pltpu.VMEM((block, D), F32),
+            pltpu.VMEM((rows, D), F32),
+            pltpu.VMEM((rows, D), F32),
         ),
         in_specs=[pl.BlockSpec(memory_space=pltpu.SMEM)] + [anywhere] * 6,
-        out_specs=(pl.BlockSpec(memory_space=pl.ANY), vmem, vmem, vmem, vmem),
+        out_specs=(vmem,) * 5,
         scratch_shapes=[
             pltpu.VMEM((rows, width), F32),
             pltpu.VMEM((rows, width), F32),
@@ -564,17 +580,17 @@
         + [pltpu.SemaphoreType.DMA((n_head - 1, pairs))] * 2
         + [pltpu.SemaphoreType.DMA((pairs,)), pltpu.SemaphoreType.DMA((6,))],
         compiler_params=pltpu.CompilerParams(
-            collective_id=0, has_side_effects=True, vmem_limit_bytes=63 * 1024 * 1024
+            collective_id=0, has_side_effects=True, vmem_limit_bytes=65000000
         ),
     )(lengths, queries, prefix_keys, prefix_value_rows, response_keys, response_values, out_grad)
     return pl.pallas_call(
         settle,
         out_shape=tuple(shape(x.shape, x.dtype) for x in results),
-        in_specs=[anywhere] * len(results),
+        in_specs=[vmem] * len(results),
         out_specs=(anywhere,) * len(results),
-        scratch_shapes=[pltpu.VMEM(x.shape, x.dtype) for x in results]
-        + [pltpu.SemaphoreType.DMA((len(results),))] * 2,
-    )(*results)
+        scratch_shapes=[pltpu.SemaphoreType.DMA((len(results),))],
+        compiler_params=pltpu.CompilerParams(vmem_limit_bytes=8 * 1024 * 1024),
+    )(*(pltpu.with_memory_space_constraint(x, pltpu.VMEM) for x in results))
 
 
 def solution(mesh):

time: 56 us -> 50.6 us (0.904)
  Pallas kernels: 54.4 us -> 49 us
    pallas_call x1, Pallas kernels: 51.9 us -> 47.8 us  [per_device(): pl.pallas_call(functools.partial(kernel, n_seq, n_head), out_shape=(pltpu...]
    pallas_call x1, Pallas kernels: 2.52 us -> 1.26 us  [per_device(): pl.pallas_call(settle, out_shape=tuple((shape(x.shape, x.dtype) for x in...]
where the time goes in v2:
time: 50.6 us; the launch traced here: 50.5 us
  Pallas kernels  49 us (97%)
  between operations  1.45 us (3%)
    pallas_call x1, Pallas kernels, per_device(): pl.pallas_call(functools.partial(kernel, n_seq, n_head), out_shape=(pltpu...  47.8 us
    pallas_call x1, Pallas kernels, per_device(): pl.pallas_call(settle, out_shape=tuple((shape(x.shape, x.dtype) for x in...  1.26 us

profile of v2, /device:TPU:0, one launch (start us, length us, event | category | flops | bytes accessed | tf_op | source)
XLA Modules:
  0.0 50.5 jit_solution(18059797398118952955)
XLA Ops:
  1.3 47.8 %shard_map.110 = (f32[32,8192]{1,0:T(8,128)S(1)}, f32[640,128]{1,0:T(8,128)S(1)}, f32[640,128]{1,0:T(8,128)S(1)}, f32[128,128]{1,0:T(8,128)S(1)}, f32[128,128]{1,0:T(8,128)S(1)}) custom-call(s32[1]{0:T(128)S(6)} %copy.12.length_ref, f32[128,2048]{1,0:T(8,128)} %q_hbm.1, f32[640,128]{1,0:T(8,128)} %pk_ref.1, f32[640,128]{1,0:T(8,128)} %pv_ref.1, ...), custom_call_target="tpu_custom_call" | custom-call | tf_op jit(solution)/shard_map/pallas_call | solution.py:540
  49.1 1.3 %shard_map.111 = (f32[32,8192]{1,0:T(8,128)}, f32[640,128]{1,0:T(8,128)}, f32[640,128]{1,0:T(8,128)}, f32[128,128]{1,0:T(8,128)}, f32[128,128]{1,0:T(8,128)}) custom-call(f32[32,8192]{1,0:T(8,128)S(1)} %get-tuple-element.10.refs_0_, f32[640,128]{1,0:T(8,128)S(1)} %get-tuple-element.11.refs_1_, f32[640,128]{1,0:T(8,128)S(1)} %get-tuple-element.12.refs_2_, ...), custom_call_target="tpu_custom_call" | custom-call | tf_op jit(solution)/shard_map/pallas_call | solution.py:586

commit v3 on v2

--- a/solution.py
+++ b/solution.py
@@ -352,19 +352,18 @@
 
     every, front, last = range(parts), range(cut), range(cut, parts)
     loops = pairs // STEP
-    assert cut - 1 <= pairs // 2 and parts > 1 + loops
-
-    relay(0, range(1))
+    assert cut - 1 <= pairs // 2 and parts > 2 * loops
+
     staggered(
         lead_products,
         lambda pair: sums(pair, 0, lead, True),
         STEP,
-        lambda i: relay(0, [i + 1]),
+        lambda i: relay(0, [i]),
     )
-    relay(0, range(1 + loops, cut))
+    relay(0, range(loops, cut))
     place_keys(kv2.at[0], 0, off2, front_size)
     key_scores(off2, front_size)
-    relay(0, range(max(1 + loops, cut), parts))
+    relay(0, range(max(loops, cut), parts))
     place_keys(kv2.at[0], last_at, off2 + last_at, last_size)
     key_scores(off2 + last_at, last_size)
     arrive(0, front)
@@ -374,7 +373,6 @@
     arrive(0, last)
     place_keys(kv1.at[0], last_at, off1 + last_at, last_size)
     key_scores(off1 + last_at, last_size)
-    relay(1, range(1, 2))
 
     def total(pair, carry):
         l = jnp.sum(l_ref[pair], axis=0, keepdims=True)
@@ -444,18 +442,17 @@
             to_peer(step, pair).start()
         keep(pair).start()
 
-    value_grads(off1, block, lambda i: relay(1, [2 + i]))
+    value_grads(off1, block, lambda i: relay(1, [1 + i]))
     send_y(1, every, odd)
-    relay(1, range(2 + loops, parts))
+    value_grads(off2, block, lambda i: relay(1, [1 + loops + i]))
+    relay(1, range(1 + 2 * loops, parts))
     send_y(1, every, even)
-    value_grads(off2, block, None)
     send_z_odd(1, every)
     place_values(kv2.at[1], 0, off2, block)
     value_scores(off2, block)
     arrive(1, front)
     place_values(kv1.at[1], 0, off1, front_size)
     value_scores(off1, front_size)
-    join(1, range(1))
     arrive(1, last)
     place_values(kv1.at[1], last_at, off1 + last_at, last_size)
     value_scores(off1 + last_at, last_size)
@@ -469,12 +466,14 @@
     quarter = pairs // 4
     key_grads(off1 + last_at, last_size, True, 0, pairs)
     send_y(0, last)
+    join(1, range(1))
+    key_grads(off1, front_size, False, 0, quarter)
+    key_grads(off2, block, False, 0, quarter)
+    lead_queries(0, quarter, stage)
     join(1, range(1, 3))
-    key_grads(off1, front_size, False, 0, pairs)
+    key_grads(off1, front_size, False, quarter, pairs)
     send_y(0, front)
     join(1, range(3, parts))
-    key_grads(off2, block, False, 0, quarter)
-    lead_queries(0, quarter, stage)
     key_grads(off2, block, False, quarter, pairs)
     send_z_odd(0, every)
     join(0, last)

time: 50.6 us -> 49.1 us (0.970)
  Pallas kernels: 49 us -> 47.5 us
    pallas_call x1, Pallas kernels: 47.8 us -> 46.3 us  [per_device(): pl.pallas_call(functools.partial(kernel, n_seq, n_head), out_shape=(pltpu...]
where the time goes in v3:
time: 49.1 us; the launch traced here: 49 us
  Pallas kernels  47.5 us (97%)
  between operations  1.45 us (3%)
    pallas_call x1, Pallas kernels, per_device(): pl.pallas_call(functools.partial(kernel, n_seq, n_head), out_shape=(pltpu...  46.3 us
    pallas_call x1, Pallas kernels, per_device(): pl.pallas_call(settle, out_shape=tuple((shape(x.shape, x.dtype) for x in...  1.26 us

profile of v3, /device:TPU:0, one launch (start us, length us, event | category | flops | bytes accessed | tf_op | source)
XLA Modules:
  0.0 49.0 jit_solution(7400956820316636137)
XLA Ops:
  1.3 46.3 %shard_map.110 = (f32[32,8192]{1,0:T(8,128)S(1)}, f32[640,128]{1,0:T(8,128)S(1)}, f32[640,128]{1,0:T(8,128)S(1)}, f32[128,128]{1,0:T(8,128)S(1)}, f32[128,128]{1,0:T(8,128)S(1)}) custom-call(s32[1]{0:T(128)S(6)} %copy.12.length_ref, f32[128,2048]{1,0:T(8,128)} %q_hbm.1, f32[640,128]{1,0:T(8,128)} %pk_ref.1, f32[640,128]{1,0:T(8,128)} %pv_ref.1, ...), custom_call_target="tpu_custom_call" | custom-call | tf_op jit(solution)/shard_map/pallas_call | solution.py:539
  47.5 1.3 %shard_map.111 = (f32[32,8192]{1,0:T(8,128)}, f32[640,128]{1,0:T(8,128)}, f32[640,128]{1,0:T(8,128)}, f32[128,128]{1,0:T(8,128)}, f32[128,128]{1,0:T(8,128)}) custom-call(f32[32,8192]{1,0:T(8,128)S(1)} %get-tuple-element.10.refs_0_, f32[640,128]{1,0:T(8,128)S(1)} %get-tuple-element.11.refs_1_, f32[640,128]{1,0:T(8,128)S(1)} %get-tuple-element.12.refs_2_, ...), custom_call_target="tpu_custom_call" | custom-call | tf_op jit(solution)/shard_map/pallas_call | solution.py:585
